TPU v7x, 32 devices: a whole 2x2x4 slice. The times are simulated.
32 devices in a mesh: prow: 4 (over x, core), pcol: 8 (over z, y).
Axes of the slice: x: 2, y: 2, z: 4, core: 2. Of those that a mesh axis runs over, the one named last changes fastest.
Arguments:
- panels: bfloat16 [2, 48, 2048, 256], P(None, 'pcol', 'prow'), may hold values from -0.59765625 to 0.59765625
- inverses: bfloat16 [2, 48, 256, 256], P(None, 'pcol', 'prow'), may hold values from -0.25 to 0.25
- dest: int32 [48, 8, 8], P('pcol', 'prow'), may hold values from 0 to 7, as said below
- target: int32 [48, 8, 8], P('pcol', 'prow'), may hold values from 0 to 1
- ancestors: float32 [2, 2048, 2048], P(None, 'prow', 'pcol'), may hold values from -6 to 6
Outputs:
- factor: bfloat16 [2, 48, 2048, 256], P(None, 'pcol', 'prow')
- schur: float32 [2, 2048, 2048], P(None, 'prow', 'pcol')
Inputs may be any that keep to these rules, and one draw needn't show every extreme that they name: `dest`: among the 96 update blocks of one device (its leaves, its block rows), at most 24 name any one process column; on every process row one process column is named by exactly 24 blocks of every device of that row.
All inputs are finite; a program needn't handle non-finite values.
Results may differ from a plain program's by a relative error of at most 0.0045.
Values may be sent and summed in bfloat16 or wider, within the bound.
No kernel may reach another device: no remote copies, remote signals or barrier semaphores. Data moves between devices by JAX's collectives and lax.ppermute only.
A program may use at most 128 MiB of HBM per device.

v0:
```python
import jax
import jax.numpy as jnp
from jax import lax
from jax.sharding import PartitionSpec as P


def complex_product(left_real, left_imag, right_real, right_imag, pattern):

    def single(first_operand, second):
        return jnp.einsum(pattern, first_operand, second, preferred_element_type=jnp.float32)

    real_part = single(left_real, right_real) - single(left_imag, right_imag)
    imag_part = single(left_real, right_imag) + single(left_imag, right_real)
    return jnp.stack([real_part, imag_part]).astype(jnp.bfloat16)


def local(panels, inverses, dest, target, ancestors):
    inverse_full = lax.all_gather(inverses, "prow", axis=2, tiled=True)
    lower_panel = complex_product(
        panels[0], panels[1], inverse_full[0], inverse_full[1], "lrk,lkc->lrc"
    )
    segment = lax.all_gather(panels, "prow", axis=2, tiled=True)
    update = complex_product(lower_panel[0], lower_panel[1], segment[0], segment[1], "lrk,lck->lrc")
    block_width = panels.shape[3]
    leaf_count = panels.shape[1]
    local_rows = panels.shape[2] // block_width
    front_blocks = update.shape[3] // block_width
    blocks = update.reshape(2, leaf_count, local_rows, block_width, front_blocks, block_width)
    blocks = blocks.transpose(1, 2, 4, 0, 3, 5).reshape(-1, 2, block_width, block_width)
    block_count = blocks.shape[0]
    column_count = lax.axis_size("pcol")
    owned_blocks = ancestors.shape[1] // block_width
    dest_flat = dest.reshape(-1)
    target_flat = target.reshape(-1)
    slot_keys = dest_flat * owned_blocks + target_flat
    select = (
        jnp.arange(column_count * owned_blocks, dtype=jnp.int32)[:, None] == slot_keys[None, :]
    ).astype(jnp.bfloat16)
    merged = jnp.dot(select, blocks.reshape(block_count, -1), preferred_element_type=jnp.float32)
    arrived = lax.all_to_all(
        merged.astype(jnp.bfloat16), "pcol", split_axis=0, concat_axis=0, tiled=True
    ).astype(merged.dtype)
    summed = jnp.sum(arrived.reshape(column_count, owned_blocks, -1), axis=0)
    summed = summed.reshape(owned_blocks, 2, block_width, block_width).transpose(1, 0, 2, 3)
    summed = summed.reshape(2, owned_blocks * block_width, block_width)
    return (lower_panel, ancestors - summed)


def solution(mesh):
    return jax.shard_map(
        local,
        mesh=mesh,
        in_specs=(
            P(None, "pcol", "prow", None),
            P(None, "pcol", "prow", None),
            P("pcol", "prow", None),
            P("pcol", "prow", None),
            P(None, "prow", "pcol"),
        ),
        out_specs=(P(None, "pcol", "prow", None), P(None, "prow", "pcol")),
        check_vma=False,
    )
```

profile of v0, /device:TPU:0, one launch (start us, length us, event | category | flops | bytes accessed | tf_op | source)
XLA Modules:
  0.0 374.9 jit_solution(875081187153657765)
XLA Ops:
  7.2 0.7 all-gather.3.cloned.1.call-update
  8.0 0.7 all-gather.5.cloned.1.call-update
  8.8 23.1 %all-gather.3.cloned.1.call-done = bf16[2,6,256,256]{3,2,1,0:T(8,128)(2,1)} async-done(((bf16[2,6,64,256]{3,2,1,0:T(8,128)(2,1)}), bf16[2,6,256,256]{3,2,1,0:T(8,128)(2,1)}) %all-gather.3.cloned.1.call-update) | async-done | bytes 1572880 | tf_op jit(solution)/shard_map/all_gather | solution.py:18
  32.0 1.8 fusion.6
  34.4 1.3 copy-done.1
  36.8 78.8 %all-gather.5.cloned.1.call-done = bf16[2,6,2048,256]{3,2,1,0:T(8,128)(2,1)} async-done(((bf16[2,6,512,256]{3,2,1,0:T(8,128)(2,1)}), bf16[2,6,2048,256]{3,2,1,0:T(8,128)(2,1)}) %all-gather.5.cloned.1.call-update) | async-done | bytes 12582928 | tf_op jit(solution)/shard_map/all_gather | solution.py:22
  115.6 12.9 %fusion.1 = f32[6,512,2048]{2,1,0:T(8,128)} fusion(bf16[6,512,256]{2,1,0:T(8,128)(2,1)S(1)} %subtract_convert_fusion.1, bf16[2,6,2048,256]{3,2,1,0:T(8,128)(2,1)} %all-gather.5.cloned.1.call-done), kind=kOutput, calls=%fused_computation.8 | convolution fusion | flops 3221225472 | bytes 33030144 | tf_op jit(solution)/shard_map/lrk,lck->lrc/dot_general | solution.py:10
  128.5 18.0 %add_convert_fusion = bf16[6,512,2048]{2,1,0:T(8,128)(2,1)} fusion(f32[6,512,2048]{2,1,0:T(8,128)} %fusion.1, bf16[6,512,256]{2,1,0:T(8,128)(2,1)S(1)} %add_convert_fusion.1, bf16[2,6,2048,256]{3,2,1,0:T(8,128)(2,1)} %all-gather.5.cloned.1.call-done), kind=kOutput, calls=%fused_computation.2 | convolution fusion | flops 3233808384 | bytes 45613056 | tf_op jit(solution)/shard_map/lrk,lck->lrc/dot_general | solution.py:10
  146.5 8.3 %copy.13 = bf16[384,8,8,256]{3,2,1,0:T(8,128)(2,1)S(1)} copy(bf16[384,8,8,256]{3,1,2,0:T(8,128)(2,1)} %bitcast.53) | data formatting | bytes 25165824
  154.8 6.0 %copy.10 = bf16[1,6,2,256,8,256]{5,3,0,4,2,1:T(8,128)(2,1)} copy(bf16[1,6,2,256,8,256]{5,4,3,2,1,0:T(8,128)(2,1)S(1)} %bitcast.54) | data formatting | bytes 25165824 | tf_op jit(solution)/shard_map/stack | solution.py:14
  160.8 12.9 %fusion = f32[6,512,2048]{2,1,0:T(8,128)} fusion(bf16[6,512,256]{2,1,0:T(8,128)(2,1)S(1)} %subtract_convert_fusion.1, bf16[2,6,2048,256]{3,2,1,0:T(8,128)(2,1)} %all-gather.5.cloned.1.call-done), kind=kOutput, calls=%fused_computation.7 | convolution fusion | flops 3221225472 | bytes 33030144 | tf_op jit(solution)/shard_map/lrk,lck->lrc/dot_general | solution.py:10
  173.7 18.1 %subtract_convert_fusion = bf16[6,512,2048]{2,1,0:T(8,128)(2,1)} fusion(f32[6,512,2048]{2,1,0:T(8,128)} %fusion, bf16[6,512,256]{2,1,0:T(8,128)(2,1)S(1)} %add_convert_fusion.1, bf16[2,6,2048,256]{3,2,1,0:T(8,128)(2,1)} %all-gather.5.cloned.1.call-done), kind=kOutput, calls=%fused_computation.3 | convolution fusion | flops 3233808384 | bytes 45613056 | tf_op jit(solution)/shard_map/lrk,lck->lrc/dot_general | solution.py:10
  191.7 9.6 %copy.12 = bf16[384,8,8,256]{3,2,1,0:T(8,128)(2,1)S(1)} copy(bf16[384,8,8,256]{3,1,2,0:T(8,128)(2,1)} %bitcast.52) | data formatting | bytes 25165824
  201.4 6.2 %copy.9 = bf16[1,6,2,256,8,256]{5,3,0,4,2,1:T(8,128)(2,1)S(1)} copy(bf16[1,6,2,256,8,256]{5,4,3,2,1,0:T(8,128)(2,1)S(1)} %bitcast.55) | data formatting | bytes 25165824 | tf_op jit(solution)/shard_map/stack | solution.py:14
  207.6 10.0 %maximum_bitcast_fusion = bf16[6,2,8,2,256,256]{5,4,3,2,1,0:T(8,128)(2,1)} fusion(bf16[1,6,2,256,8,256]{5,3,0,4,2,1:T(8,128)(2,1)S(1)} %bitcast.57, bf16[1,6,2,256,8,256]{5,3,0,4,2,1:T(8,128)(2,1)S(1)} %copy.9), kind=kLoop, calls=%fused_computation.1 | loop fusion | flops 12582912 | bytes 50331648 | tf_op jit(solution)/shard_map/transpose | solution.py:29
  217.6 25.1 %reshape_reshape.3 = bf16[96,131072]{1,0:T(8,128)(2,1)} reshape(bf16[6,2,8,2,256,256]{5,4,3,2,1,0:T(8,128)(2,1)} %maximum_bitcast_fusion) | data formatting | bytes 50331648 | tf_op jit(solution)/shard_map/reshape;reshape | solution.py:39
  242.7 12.0 %convolution_convert_fusion = bf16[16,131072]{1,0:T(8,128)(2,1)} fusion(bf16[96,131072]{1,0:T(8,128)(2,1)} %reshape_reshape.3, s32[96]{0:T(128)S(1)} %add.18), kind=kOutput, calls=%fused_computation | convolution fusion | flops 404751872 | bytes 29360512 | tf_op jit(solution)/shard_map/dot_general | solution.py:39
  254.7 5.5 %all_to_all.6 = bf16[8,2,131072]{2,1,0:T(2,128)(2,1)} reshape(bf16[16,131072]{1,0:T(8,128)(2,1)} %convolution_convert_fusion) | data formatting | bytes 8388608 | tf_op jit(solution)/shard_map/all_to_all | solution.py:40
  260.2 5.5 %all-to-all-start = ((bf16[8,2,131072]{2,1,0:T(2,128)(2,1)}), bf16[8,2,131072]{2,1,0:T(2,128)(2,1)}, u32[]{:S(2)}, u32[]{:S(2)}) async-start(bf16[8,2,131072]{2,1,0:T(2,128)(2,1)} %all_to_all.6), calls=%async_computation | async-start | bytes 8388608 | tf_op jit(solution)/shard_map/all_to_all | solution.py:40
  265.7 1.9 pad_maximum_fusion
  267.7 91.8 %all-to-all-done = bf16[8,2,131072]{2,1,0:T(2,128)(2,1)} async-done(((bf16[8,2,131072]{2,1,0:T(2,128)(2,1)}), bf16[8,2,131072]{2,1,0:T(2,128)(2,1)}, u32[]{:S(2)}, u32[]{:S(2)}) %all-to-all-start) | async-done | bytes 4194336 | tf_op jit(solution)/shard_map/all_to_all | solution.py:40
  359.4 6.3 %convert_reduce_fusion = f32[2,131072]{1,0:T(2,128)S(1)} fusion(bf16[8,2,131072]{2,1,0:T(2,128)(2,1)} %all-to-all-done), kind=kLoop, calls=%fused_computation.4 | loop fusion | flops 3932160 | bytes 5242880 | tf_op jit(solution)/shard_map/reduce_sum | solution.py:43
  365.9 1.1 copy-done.3
  367.0 1.1 bitcast_subtract_fusion
  (26 shorter events, 2.1 us)
Async XLA Ops:
  7.2 24.8 %copy-start = (bf16[2,6,512,256]{3,2,1,0:T(8,128)(2,1)S(1)}, bf16[2,6,512,256]{3,2,1,0:T(8,128)(2,1)}, u32[]{:S(2)}) copy-start(bf16[2,6,512,256]{3,2,1,0:T(8,128)(2,1)} %param.5) | copy-start | bytes 9437188
  7.2 1.5 copy-start.5
  7.2 1.5 copy-start.4
  7.2 24.8 %all-gather.3.cloned.1.call-start = ((), (), s32[]{:S(2)}) async-start(), calls=%async_computation.1 | async-start | bytes 1966080 | tf_op jit(solution)/shard_map/all_gather | solution.py:18
  7.9 107.7 %all-gather.5.cloned.1.call-start = ((), (), s32[]{:S(2)}) async-start(), calls=%async_computation.2 | async-start | bytes 15728640 | tf_op jit(solution)/shard_map/all_gather | solution.py:22
  32.0 1.8 copy-start.2
  33.8 1.9 copy-start.1
  191.7 15.8 %slice-start = ((s8[12582912]{0:T(1024)(128)(4,1)}), s8[4194304]{0:T(1024)(128)(4,1)S(1)}, s32[]{:S(2)}) async-start(s8[12582912]{0:T(1024)(128)(4,1)} %bitcast.56), calls=%async_computation.3 | async-start | bytes 8388608
  191.7 15.8 %slice-start.1 = ((s8[12582912]{0:T(1024)(128)(4,1)}), s8[4194304]{0:T(1024)(128)(4,1)S(1)}, s32[]{:S(2)}) async-start(s8[12582912]{0:T(1024)(128)(4,1)} %bitcast.56), calls=%async_computation.4 | async-start | bytes 8388608
  201.4 6.2 %slice-start.2 = ((s8[12582912]{0:T(1024)(128)(4,1)}), s8[4194304]{0:T(1024)(128)(4,1)S(1)}, s32[]{:S(2)}) async-start(s8[12582912]{0:T(1024)(128)(4,1)} %bitcast.56), calls=%async_computation.5 | async-start | bytes 8388608
  260.2 99.2 %all-to-all-start = ((bf16[8,2,131072]{2,1,0:T(2,128)(2,1)}), bf16[8,2,131072]{2,1,0:T(2,128)(2,1)}, u32[]{:S(2)}, u32[]{:S(2)}) async-start(bf16[8,2,131072]{2,1,0:T(2,128)(2,1)} %all_to_all.6), calls=%async_computation | async-start | bytes 8388608 | tf_op jit(solution)/shard_map/all_to_all | solution.py:40
  365.7 1.2 copy-start.3
Sparse Core Ops, SparseCore 0:
  9.6 22.3 all-gather.2
  33.5 82.0 all-gather.4
where the time goes:
time: 376 us; the launch traced here: 375 us
  waiting for transfers between devices  195 us (52%)
  matrix products  77.3 us (21%)
  local copies, waits for them, and re-layouts  63.4 us (17%)
  other arithmetic  19.3 us (5%)
  between operations  14.2 us (4%)
  starting transfers between devices  5.59 us (1%)
    all_to_all x1, waiting for transfers between devices, local(): lax.all_to_all(merged.astype(jnp.bfloat16), 'pcol', split_axis=0, concat_...  91.8 us
    all_gather x1, waiting for transfers between devices, local(): segment = lax.all_gather(panels, 'prow', axis=2, tiled=True)  78.8 us
    dot_general x8, matrix products, single(): jnp.einsum(pattern, first_operand, second, preferred_element_type=jnp.flo...  65.3 us
    another operation x1, local copies, waits for them, and re-layouts, local(): blocks.reshape(block_count, -1)  25.1 us
    all_gather x1, waiting for transfers between devices, local(): inverse_full = lax.all_gather(inverses, 'prow', axis=2, tiled=True)  23.1 us
    unnamed x21, local copies, waits for them, and re-layouts  20.4 us
    another operation x2, local copies, waits for them, and re-layouts, complex_product(): return jnp.stack([real_part, imag_part]).astype(jnp.bfloat16)  12.2 us
    dot_general x1, matrix products, local(): jnp.dot(select, blocks.reshape(block_count, -1), preferred_element_type=j...  12 us
  transfers between devices with their start and end apart: 3, of which 3 were waited for; matrix products, arithmetic and copies ran while one was open for 1% of the time, Pallas kernels for 0%

commit v1 on v0

--- a/solution.py
+++ b/solution.py
@@ -2,6 +2,22 @@
 import jax.numpy as jnp
 from jax import lax
 from jax.sharding import PartitionSpec as P
+
+
+def gather_around(x, axis, dim):
+    ways, here, step = (lax.axis_size(axis), lax.axis_index(axis), x.shape[dim])
+    dims = [n * ways if d == dim else n for d, n in enumerate(x.shape)]
+    full = lax.dynamic_update_slice_in_dim(jnp.zeros(dims, x.dtype), x, here * step, axis=dim)
+    going_up = going_down = x
+    for far in range(1, ways // 2 + 1):
+        going_up = lax.ppermute(going_up, axis, [(d, (d + 1) % ways) for d in range(ways)])
+        full = lax.dynamic_update_slice_in_dim(full, going_up, (here - far) % ways * step, axis=dim)
+        if 2 * far < ways:
+            going_down = lax.ppermute(going_down, axis, [(d, (d - 1) % ways) for d in range(ways)])
+            full = lax.dynamic_update_slice_in_dim(
+                full, going_down, (here + far) % ways * step, axis=dim
+            )
+    return full
 
 
 def complex_product(left_real, left_imag, right_real, right_imag, pattern):
@@ -15,7 +31,7 @@
 
 
 def local(panels, inverses, dest, target, ancestors):
-    inverse_full = lax.all_gather(inverses, "prow", axis=2, tiled=True)
+    inverse_full = gather_around(inverses, "prow", 2)
     lower_panel = complex_product(
         panels[0], panels[1], inverse_full[0], inverse_full[1], "lrk,lkc->lrc"
     )

time: 376 us -> 338 us (0.90)
  waiting for transfers between devices: 195 us -> 120 us
  local copies, waits for them, and re-layouts: 63.4 us -> 97.1 us
  starting transfers between devices: 5.59 us -> 12.2 us
  matrix products: 77.3 us -> 73.2 us
    all_gather x1, waiting for transfers between devices: 78.8 us -> 25.3 us  [local(): segment = lax.all_gather(panels, 'prow', axis=2, tiled=True)]
    dynamic_update_slice x0 -> x4, local copies, waits for them, and re-layouts: none -> 34.1 us  [the longest x2 16.3 us: gather_around(): lax.dynamic_update_slice_in_dim(full, going_up, (here - far) % ways * ste...]
    all_gather x1 -> x0, waiting for transfers between devices: 23.1 us -> none  [local(): inverse_full = lax.all_gather(inverses, 'prow', axis=2, tiled=True)]
    unnamed x21 -> x23, local copies, waits for them, and re-layouts: 20.4 us -> 12.9 us
    ppermute x0 -> x3, waiting for transfers between devices: none -> 7.18 us  [the longest x2 7.18 us: gather_around(): lax.ppermute(going_up, axis, [(d, (d + 1) % ways) for d in range(ways)])]
    ppermute x0 -> x3, local copies, waits for them, and re-layouts: none -> 5.82 us  [the longest x2 3.52 us: gather_around(): lax.ppermute(going_up, axis, [(d, (d + 1) % ways) for d in range(ways)])]
    ppermute x0 -> x3, starting transfers between devices: none -> 4.82 us  [the longest x2 2.9 us: gather_around(): lax.ppermute(going_up, axis, [(d, (d + 1) % ways) for d in range(ways)])]
    all_to_all x1, waiting for transfers between devices: 91.8 us -> 87.1 us  [local(): lax.all_to_all(merged.astype(jnp.bfloat16), 'pcol', split_axis=0, concat_...]
  transfers between devices with their start and end apart: 3 -> 5, of which waited for: 3 -> 3; matrix products, arithmetic and copies ran while one was open for 1% -> 16% of each run, Pallas kernels for 0% -> 0%
where the time goes in v1:
time: 338 us; the launch traced here: 337 us
  waiting for transfers between devices  120 us (36%)
  local copies, waits for them, and re-layouts  97.1 us (29%)
  matrix products  73.2 us (22%)
  other arithmetic  19.4 us (6%)
  between operations  14.3 us (4%)
  starting transfers between devices  12.2 us (4%)
    all_to_all x1, waiting for transfers between devices, local(): lax.all_to_all(merged.astype(jnp.bfloat16), 'pcol', split_axis=0, concat_...  87.1 us
    dot_general x8, matrix products, single(): jnp.einsum(pattern, first_operand, second, preferred_element_type=jnp.flo...  61.2 us
    all_gather x1, waiting for transfers between devices, local(): segment = lax.all_gather(panels, 'prow', axis=2, tiled=True)  25.3 us
    another operation x1, local copies, waits for them, and re-layouts, local(): blocks.reshape(block_count, -1)  25.1 us
    dynamic_update_slice x2, local copies, waits for them, and re-layouts, gather_around(): lax.dynamic_update_slice_in_dim(full, going_up, (here - far) % ways * ste...  16.3 us
    unnamed x23, local copies, waits for them, and re-layouts  12.9 us
    another operation x2, local copies, waits for them, and re-layouts, complex_product(): return jnp.stack([real_part, imag_part]).astype(jnp.bfloat16)  12.2 us
    dot_general x1, matrix products, local(): jnp.dot(select, blocks.reshape(block_count, -1), preferred_element_type=j...  12 us
  transfers between devices with their start and end apart: 5, of which 3 were waited for; matrix products, arithmetic and copies ran while one was open for 16% of the time, Pallas kernels for 0%

profile of v1, /device:TPU:0, one launch (start us, length us, event | category | flops | bytes accessed | tf_op | source)
XLA Modules:
  0.0 336.5 jit_solution(9535907985160029140)
XLA Ops:
  10.6 7.2 %collective-permute-done = bf16[2,6,64,256]{3,2,1,0:T(8,128)(2,1)} collective-permute-done((bf16[2,6,64,256]{3,2,1,0:T(8,128)(2,1)S(1)}, bf16[2,6,64,256]{3,2,1,0:T(8,128)(2,1)}, u32[]{:S(2)}, u32[]{:S(2)}) %collective-permute-start) | collective-permute-done | bytes 393248 | tf_op jit(solution)/shard_map/ppermute | solution.py:13
  17.7 2.4 collective-permute-start.2
  22.0 8.0 %dynamic_update_slice.12 = bf16[2,6,256,256]{2,3,1,0:T(8,128)(2,1)} dynamic-update-slice(bf16[2,6,256,256]{2,3,1,0:T(8,128)(2,1)} %broadcast_in_dim.2, bf16[2,6,64,256]{2,3,1,0:T(8,128)(2,1)S(1)} %copy.36, s32[]{:T(128)} %constant.33.clone.1, s32[]{:T(128)} %constant.33.clone.1, s32[]{:T(128)S(6)} %select_n.27, s32[]{:T(128)} %constant.33.clone.1) | dynamic-update-slice | bytes 786436 | tf_op jit(solution)/shard_map/dynamic_update_slice | solution.py:10
  31.3 8.7 %dynamic_update_slice.13 = bf16[2,6,256,256]{2,3,1,0:T(8,128)(2,1)} dynamic-update-slice(bf16[2,6,256,256]{2,3,1,0:T(8,128)(2,1)} %dynamic_update_slice.12, bf16[2,6,64,256]{2,3,1,0:T(8,128)(2,1)S(1)} %copy.37, s32[]{:T(128)} %constant.33.clone.1, s32[]{:T(128)} %constant.33.clone.1, s32[]{:T(128)S(6)} %select_n.29, s32[]{:T(128)} %constant.33.clone.1) | dynamic-update-slice | bytes 786436 | tf_op jit(solution)/shard_map/dynamic_update_slice | solution.py:14
  40.1 2.3 copy.38
  42.4 9.8 %dynamic_update_slice.14 = bf16[2,6,256,256]{2,3,1,0:T(8,128)(2,1)} dynamic-update-slice(bf16[2,6,256,256]{2,3,1,0:T(8,128)(2,1)} %dynamic_update_slice.13, bf16[2,6,64,256]{2,3,1,0:T(8,128)(2,1)} %copy.38, s32[]{:T(128)} %constant.33.clone.1, s32[]{:T(128)} %constant.33.clone.1, s32[]{:T(128)S(6)} %select_n.31, s32[]{:T(128)} %constant.33.clone.1) | dynamic-update-slice | bytes 786436 | tf_op jit(solution)/shard_map/dynamic_update_slice | solution.py:17
  54.4 7.5 %dynamic_update_slice.15 = bf16[2,6,256,256]{2,3,1,0:T(8,128)(2,1)} dynamic-update-slice(bf16[2,6,256,256]{2,3,1,0:T(8,128)(2,1)} %dynamic_update_slice.14, bf16[2,6,64,256]{2,3,1,0:T(8,128)(2,1)} %copy.39, s32[]{:T(128)} %constant.33.clone.1, s32[]{:T(128)} %constant.33.clone.1, s32[]{:T(128)S(6)} %select_n.33, s32[]{:T(128)} %constant.33.clone.1) | dynamic-update-slice | bytes 786436 | tf_op jit(solution)/shard_map/dynamic_update_slice | solution.py:14
  69.3 25.3 %all-gather.2.cloned.1.call-done = bf16[2,6,2048,256]{3,2,1,0:T(8,128)(2,1)} async-done(((bf16[2,6,512,256]{3,2,1,0:T(8,128)(2,1)}), bf16[2,6,2048,256]{3,2,1,0:T(8,128)(2,1)}) %all-gather.2.cloned.1.call-update) | async-done | bytes 12582928 | tf_op jit(solution)/shard_map/all_gather | solution.py:38
  94.6 12.9 %fusion = f32[6,512,2048]{2,1,0:T(8,128)} fusion(bf16[6,256,512]{2,1,0:T(8,128)(2,1)S(1)} %subtract_convert_fusion.1, bf16[2,6,2048,256]{3,2,1,0:T(8,128)(2,1)} %all-gather.2.cloned.1.call-done), kind=kOutput, calls=%fused_computation.7 | convolution fusion | flops 3221225472 | bytes 33030144 | tf_op jit(solution)/shard_map/lrk,lck->lrc/dot_general | solution.py:26
  107.5 14.2 %subtract_convert_fusion = bf16[6,512,2048]{2,1,0:T(8,128)(2,1)S(1)} fusion(f32[6,512,2048]{2,1,0:T(8,128)} %fusion, bf16[6,256,512]{2,1,0:T(8,128)(2,1)S(1)} %add_convert_fusion.1, bf16[2,6,2048,256]{3,2,1,0:T(8,128)(2,1)} %all-gather.2.cloned.1.call-done), kind=kOutput, calls=%fused_computation.3 | convolution fusion | flops 3233808384 | bytes 45613056 | tf_op jit(solution)/shard_map/lrk,lck->lrc/dot_general | solution.py:26
  121.7 3.2 copy.52
  124.9 6.0 %copy.44 = bf16[1,6,2,256,8,256]{5,3,0,4,2,1:T(8,128)(2,1)} copy(bf16[1,6,2,256,8,256]{5,4,3,2,1,0:T(8,128)(2,1)S(1)} %bitcast.56) | data formatting | bytes 25165824 | tf_op jit(solution)/shard_map/stack | solution.py:30
  130.8 12.9 %fusion.1 = f32[6,512,2048]{2,1,0:T(8,128)} fusion(bf16[6,256,512]{2,1,0:T(8,128)(2,1)S(1)} %subtract_convert_fusion.1, bf16[2,6,2048,256]{3,2,1,0:T(8,128)(2,1)} %all-gather.2.cloned.1.call-done), kind=kOutput, calls=%fused_computation.8 | convolution fusion | flops 3221225472 | bytes 33030144 | tf_op jit(solution)/shard_map/lrk,lck->lrc/dot_general | solution.py:26
  143.7 14.2 %add_convert_fusion = bf16[6,512,2048]{2,1,0:T(8,128)(2,1)S(1)} fusion(f32[6,512,2048]{2,1,0:T(8,128)} %fusion.1, bf16[6,256,512]{2,1,0:T(8,128)(2,1)S(1)} %add_convert_fusion.1, bf16[2,6,2048,256]{3,2,1,0:T(8,128)(2,1)} %all-gather.2.cloned.1.call-done), kind=kOutput, calls=%fused_computation.2 | convolution fusion | flops 3233808384 | bytes 45613056 | tf_op jit(solution)/shard_map/lrk,lck->lrc/dot_general | solution.py:26
  157.9 3.2 copy.53
  161.1 6.2 %copy.45 = bf16[1,6,2,256,8,256]{5,3,0,4,2,1:T(8,128)(2,1)S(1)} copy(bf16[1,6,2,256,8,256]{5,4,3,2,1,0:T(8,128)(2,1)S(1)} %bitcast.57) | data formatting | bytes 25165824 | tf_op jit(solution)/shard_map/stack | solution.py:30
  167.4 10.0 %maximum_bitcast_fusion = bf16[6,2,8,2,256,256]{5,4,3,2,1,0:T(8,128)(2,1)} fusion(bf16[1,6,2,256,8,256]{5,3,0,4,2,1:T(8,128)(2,1)S(1)} %copy.45, bf16[1,6,2,256,8,256]{5,3,0,4,2,1:T(8,128)(2,1)S(1)} %bitcast.59), kind=kLoop, calls=%fused_computation.1 | loop fusion | flops 12582912 | bytes 50331648 | tf_op jit(solution)/shard_map/transpose | solution.py:45
  177.3 25.1 %reshape_reshape.3 = bf16[96,131072]{1,0:T(8,128)(2,1)} reshape(bf16[6,2,8,2,256,256]{5,4,3,2,1,0:T(8,128)(2,1)} %maximum_bitcast_fusion) | data formatting | bytes 50331648 | tf_op jit(solution)/shard_map/reshape;reshape | solution.py:55
  202.4 12.0 %convolution_convert_fusion = bf16[16,131072]{1,0:T(8,128)(2,1)} fusion(bf16[96,131072]{1,0:T(8,128)(2,1)} %reshape_reshape.3, s32[96]{0:T(128)S(1)} %add.57), kind=kOutput, calls=%fused_computation | convolution fusion | flops 404751872 | bytes 29360512 | tf_op jit(solution)/shard_map/dot_general | solution.py:55
  214.4 5.5 %all_to_all.6 = bf16[8,2,131072]{2,1,0:T(2,128)(2,1)} reshape(bf16[16,131072]{1,0:T(8,128)(2,1)} %convolution_convert_fusion) | data formatting | bytes 8388608 | tf_op jit(solution)/shard_map/all_to_all | solution.py:56
  220.0 7.4 %all-to-all-start = ((bf16[8,2,131072]{2,1,0:T(2,128)(2,1)}), bf16[8,2,131072]{2,1,0:T(2,128)(2,1)}, u32[]{:S(2)}, u32[]{:S(2)}) async-start(bf16[8,2,131072]{2,1,0:T(2,128)(2,1)} %all_to_all.6), calls=%async_computation | async-start | bytes 8388608 | tf_op jit(solution)/shard_map/all_to_all | solution.py:56
  229.3 4.6 %copy.47 = bf16[2,6,512,256]{3,2,1,0:T(8,128)(2,1)} copy(bf16[2,6,512,256]{2,3,1,0:T(8,128)(2,1)} %pad_maximum_fusion) | data formatting | bytes 6291456
  234.0 87.1 %all-to-all-done = bf16[8,2,131072]{2,1,0:T(2,128)(2,1)} async-done(((bf16[8,2,131072]{2,1,0:T(2,128)(2,1)}), bf16[8,2,131072]{2,1,0:T(2,128)(2,1)}, u32[]{:S(2)}, u32[]{:S(2)}) %all-to-all-start) | async-done | bytes 4194336 | tf_op jit(solution)/shard_map/all_to_all | solution.py:56
  321.0 6.3 %convert_reduce_fusion = f32[2,131072]{1,0:T(2,128)S(1)} fusion(bf16[8,2,131072]{2,1,0:T(2,128)(2,1)} %all-to-all-done), kind=kLoop, calls=%fused_computation.4 | loop fusion | flops 3932160 | bytes 5242880 | tf_op jit(solution)/shard_map/reduce_sum | solution.py:59
  (39 shorter events, 20.3 us)
Async XLA Ops:
  7.2 1.0 copy-start.3
  7.2 13.4 %copy-start.5 = (s32[6,2,8]{2,1,0:T(2,128)S(1)}, s32[6,2,8]{2,1,0:T(2,128)}, u32[]{:S(2)}) copy-start(s32[6,2,8]{2,1,0:T(2,128)} %param.7) | copy-start | bytes 1156
  7.2 13.4 %copy-start.4 = (s32[6,2,8]{2,1,0:T(2,128)S(1)}, s32[6,2,8]{2,1,0:T(2,128)}, u32[]{:S(2)}) copy-start(s32[6,2,8]{2,1,0:T(2,128)} %param.8) | copy-start | bytes 1156
  7.2 87.4 %all-gather.2.cloned.1.call-start = ((), (), s32[]{:S(2)}) async-start(), calls=%async_computation.1 | async-start | bytes 15728640 | tf_op jit(solution)/shard_map/all_gather | solution.py:38
  8.2 9.6 %collective-permute-start = (bf16[2,6,64,256]{3,2,1,0:T(8,128)(2,1)S(1)}, bf16[2,6,64,256]{3,2,1,0:T(8,128)(2,1)}, u32[]{:S(2)}, u32[]{:S(2)}) collective-permute-start(bf16[2,6,64,256]{3,2,1,0:T(8,128)(2,1)S(1)} %copy-done.3), channel_id=1, source_target_pairs={{0,8},{8,16},{16,24},{24,0},{1,9},{9,17},{17,25},{25,1},{2,10},{10... | collective-permute-start | bytes 1179656 | tf_op jit(solution)/shard_map/ppermute | solution.py:13
  8.7 31.4 %collective-permute-start.1 = (bf16[2,6,64,256]{3,2,1,0:T(8,128)(2,1)S(1)}, bf16[2,6,64,256]{3,2,1,0:T(8,128)(2,1)}, u32[]{:S(2)}, u32[]{:S(2)}) collective-permute-start(bf16[2,6,64,256]{3,2,1,0:T(8,128)(2,1)S(1)} %copy-done.3), channel_id=1, source_target_pairs={{0,24},{8,0},{16,8},{24,16},{1,25},{9,1},{17,9},{25,17},{2,26},{10... | collective-permute-start | bytes 1179656 | tf_op jit(solution)/shard_map/ppermute | solution.py:16
  17.7 34.5 %collective-permute-start.2 = (bf16[2,6,64,256]{3,2,1,0:T(8,128)(2,1)}, bf16[2,6,64,256]{3,2,1,0:T(8,128)(2,1)}, u32[]{:S(2)}, u32[]{:S(2)}) collective-permute-start(bf16[2,6,64,256]{3,2,1,0:T(8,128)(2,1)} %collective-permute-done), channel_id=1, source_target_pairs={{0,8},{8,16},{16,24},{24,0},{1,9},{9,17},{17,25},{25,1},{2,10},{10... | collective-permute-start | bytes 1179656 | tf_op jit(solution)/shard_map/ppermute | solution.py:13
  40.1 21.8 %copy-start = (bf16[2,6,512,256]{3,2,1,0:T(8,128)(2,1)S(1)}, bf16[2,6,512,256]{3,2,1,0:T(8,128)(2,1)}, u32[]{:S(2)}) copy-start(bf16[2,6,512,256]{3,2,1,0:T(8,128)(2,1)} %param.5) | copy-start | bytes 9437188
  63.6 2.1 copy-start.1
  157.9 9.4 %slice-start = ((s8[12582912]{0:T(1024)(128)(4,1)}), s8[4194304]{0:T(1024)(128)(4,1)S(1)}, s32[]{:S(2)}) async-start(s8[12582912]{0:T(1024)(128)(4,1)} %bitcast.58), calls=%async_computation.2 | async-start | bytes 8388608
  157.9 9.4 %slice-start.1 = ((s8[12582912]{0:T(1024)(128)(4,1)}), s8[4194304]{0:T(1024)(128)(4,1)S(1)}, s32[]{:S(2)}) async-start(s8[12582912]{0:T(1024)(128)(4,1)} %bitcast.58), calls=%async_computation.3 | async-start | bytes 8388608
  161.1 6.2 %slice-start.2 = ((s8[12582912]{0:T(1024)(128)(4,1)}), s8[4194304]{0:T(1024)(128)(4,1)S(1)}, s32[]{:S(2)}) async-start(s8[12582912]{0:T(1024)(128)(4,1)} %bitcast.58), calls=%async_computation.4 | async-start | bytes 8388608
  220.0 101.1 %all-to-all-start = ((bf16[8,2,131072]{2,1,0:T(2,128)(2,1)}), bf16[8,2,131072]{2,1,0:T(2,128)(2,1)}, u32[]{:S(2)}, u32[]{:S(2)}) async-start(bf16[8,2,131072]{2,1,0:T(2,128)(2,1)} %all_to_all.6), calls=%async_computation | async-start | bytes 8388608 | tf_op jit(solution)/shard_map/all_to_all | solution.py:56
  327.3 1.2 copy-start.2
Sparse Core Ops, SparseCore 0:
  9.6 85.0 all-gather.1
